TPU v7x, 128 devices: a whole 4x4x4 slice. The times are simulated.
128 devices in a mesh: ctx: 32 (over y, z, core), head: 4 (over x).
Axes of the slice: x: 4, y: 4, z: 4, core: 2. Of those that a mesh axis runs over, the one named last changes fastest.
Arguments:
- query: bfloat16 [65536, 2048], P('ctx', 'head'), may hold values from -6 to 6
- key: bfloat16 [65536, 2048], P('ctx', 'head'), may hold values from -6 to 6
- value: bfloat16 [65536, 2048], P('ctx', 'head'), may hold values from -6 to 6
- gain: bfloat16 [2048], P('head'), may hold values from 0.099609375 to 1.8984375
- w_out: bfloat16 [2048, 2048], replicated, may hold values from -0.125 to 0.125
- d_out: bfloat16 [65536, 2048], P(('ctx', 'head')), may hold values from -6 to 6
Outputs:
- out: bfloat16 [65536, 2048], P(('ctx', 'head'))
- grad_query: bfloat16 [65536, 2048], P('ctx', 'head')
- grad_key: bfloat16 [65536, 2048], P('ctx', 'head')
- grad_value: bfloat16 [65536, 2048], P('ctx', 'head')
All inputs are finite; a program needn't handle non-finite values.
Results may differ from a plain program's by a relative error of at most 0.018.
Values may be sent and summed in bfloat16 or wider, within the bound.
A program may use at most 128 MiB of HBM per device.

v0:
```python
import jax
import jax.numpy as jnp
from jax import lax
from jax.sharding import Mesh
from jax.sharding import PartitionSpec as P

HDIM = 128
BLOCK = 128
CTX = ("ctx_0", "ctx_1", "ctx_2")
CTX_HEAD = ("ctx_0", "ctx_1", "ctx_2", "head")
epsilon = 1e-06


def nothing_yet(value, identity):
    return jnp.broadcast_to(jnp.asarray(identity, value.dtype), value.shape)


def prefix_by_axis(value, axes, combine, identity, reverse):
    before = start = nothing_yet(value, identity)
    total = value
    for axis in reversed(axes):
        length, mine = (lax.axis_size(axis), lax.axis_index(axis))
        pieces = lax.all_gather(total.astype(jnp.bfloat16), axis)
        inside, total = (start, start)
        for k in reversed(range(length)) if reverse else range(length):
            passed = k > mine if reverse else k < mine
            total = combine(total, pieces[k].astype(value.dtype))
            inside = jnp.where(passed, total, inside)
        before = combine(inside, before)
    return before


def add_states(earlier, later):
    return earlier + later


def earlier_states(local_total):
    return prefix_by_axis(local_total, CTX, add_states, jnp.zeros_like(local_total), False)


def later_states(local_total):
    return prefix_by_axis(local_total, CTX, add_states, jnp.zeros_like(local_total), True)


def on_device(query, key, value, gain, w_out, d_out):
    tokens, width = query.shape
    local_heads = width // HDIM
    nblocks = tokens // BLOCK
    causal = jnp.tril(jnp.ones((BLOCK, BLOCK), dtype=bool))[None, None]

    def split_blocks(array):
        return array.reshape(nblocks, BLOCK, local_heads, HDIM)

    def masked(scores):
        return jnp.where(causal, scores, jnp.zeros_like(scores)).astype(jnp.bfloat16)

    q_blocks = split_blocks(query)
    k_blocks = split_blocks(key)
    v_blocks = split_blocks(value)
    scores = masked(
        jnp.einsum("cshe,cthe->chst", q_blocks, k_blocks, preferred_element_type=jnp.float32)
    )
    block_states = jnp.einsum(
        "cshe,cshf->chef", k_blocks, v_blocks, preferred_element_type=jnp.float32
    )
    before = earlier_states(jnp.sum(block_states, axis=0))
    running = jnp.cumsum(block_states, axis=0)
    inner_before = jnp.concatenate([jnp.zeros_like(running[:1]), running[:-1]], axis=0)
    prefixes = (before[None] + inner_before).astype(jnp.bfloat16)
    attended = jnp.einsum("chst,cthf->cshf", scores, v_blocks, preferred_element_type=jnp.float32)
    attended = attended + jnp.einsum(
        "cshe,chef->cshf", q_blocks, prefixes, preferred_element_type=jnp.float32
    )
    attended = attended.reshape(tokens, local_heads, HDIM)
    inverse = lax.rsqrt(jnp.mean(attended * attended, axis=-1, keepdims=True) + epsilon)
    unit = attended * inverse
    scales = gain.astype(jnp.float32).reshape(local_heads, HDIM)
    normed = (unit * scales).astype(jnp.bfloat16).reshape(tokens, width)
    w_slice = lax.dynamic_slice_in_dim(w_out, lax.axis_index("head") * width, width, 0)
    out = lax.psum_scatter(
        jnp.dot(normed, w_slice, preferred_element_type=jnp.float32).astype(jnp.bfloat16),
        "head",
        scatter_dimension=0,
        tiled=True,
    )
    grad_heads = lax.dot_general(
        lax.all_gather(d_out, "head", axis=0, tiled=True),
        w_slice,
        (((1,), (1,)), ((), ())),
        preferred_element_type=jnp.float32,
    ).astype(jnp.bfloat16)
    grad_unit = grad_heads.astype(jnp.float32).reshape(tokens, local_heads, HDIM) * scales
    grad_attended = inverse * (
        grad_unit - unit * jnp.mean(grad_unit * unit, axis=-1, keepdims=True)
    )
    g_blocks = split_blocks(grad_attended.astype(jnp.bfloat16))
    grad_scores = masked(
        jnp.einsum("cshf,cthf->chst", g_blocks, v_blocks, preferred_element_type=jnp.float32)
    )
    block_grads = jnp.einsum(
        "cshe,cshf->chef", q_blocks, g_blocks, preferred_element_type=jnp.float32
    )
    after = later_states(jnp.sum(block_grads, axis=0))
    tail_sums = jnp.cumsum(block_grads[::-1], axis=0)[::-1]
    inner_after = jnp.concatenate([tail_sums[1:], jnp.zeros_like(tail_sums[:1])], axis=0)
    suffixes = (after[None] + inner_after).astype(jnp.bfloat16)
    grad_query = jnp.einsum(
        "chst,cthe->cshe", grad_scores, k_blocks, preferred_element_type=jnp.float32
    )
    grad_query = grad_query + jnp.einsum(
        "cshf,chef->cshe", g_blocks, prefixes, preferred_element_type=jnp.float32
    )
    grad_key = jnp.einsum(
        "chst,cshe->cthe", grad_scores, q_blocks, preferred_element_type=jnp.float32
    )
    grad_key = grad_key + jnp.einsum(
        "cthf,chef->cthe", v_blocks, suffixes, preferred_element_type=jnp.float32
    )
    grad_value = jnp.einsum("chst,cshf->cthf", scores, g_blocks, preferred_element_type=jnp.float32)
    grad_value = grad_value + jnp.einsum(
        "cthe,chef->cthf", k_blocks, suffixes, preferred_element_type=jnp.float32
    )
    return (
        out,
        grad_query.reshape(tokens, width).astype(jnp.bfloat16),
        grad_key.reshape(tokens, width).astype(jnp.bfloat16),
        grad_value.reshape(tokens, width).astype(jnp.bfloat16),
    )


def solution(mesh):
    finer = Mesh(
        mesh.devices.reshape(4, 4, 2, mesh.shape["head"]), ("ctx_0", "ctx_1", "ctx_2", "head")
    )
    in_specs = (P(CTX, "head"), P(CTX, "head"), P(CTX, "head"), P("head"), P(), P(CTX_HEAD, None))
    out_specs = (P(CTX_HEAD, None), P(CTX, "head"), P(CTX, "head"), P(CTX, "head"))
    return jax.shard_map(
        on_device, mesh=finer, in_specs=in_specs, out_specs=out_specs, check_vma=False
    )
```

profile of v0, /device:TPU:0, one launch (start us, length us, event | category | flops | bytes accessed | tf_op | source)
XLA Modules:
  0.0 214.9 jit_solution(12444934481127085550)
XLA Ops:
  7.2 0.0 all-gather.4.cloned.1.call-start
  7.2 0.7 all-gather.4.cloned.1.call-update
  7.9 0.0 reduce-scatter.2.cloned.1.call-start
  8.0 2.6 %reshape.94 = bf16[16,128,4,128]{3,2,1,0:T(4,128)(2,1)S(1)} reshape(bf16[2048,512]{1,0:T(8,128)(2,1)} %param.6) | data formatting | bytes 4194304 | tf_op jit(solution)/shard_map/reshape | solution.py:52
  10.5 4.0 %reshape.95 = bf16[16,128,4,128]{3,2,1,0:T(4,128)(2,1)} reshape(bf16[2048,512]{1,0:T(8,128)(2,1)} %param.7) | data formatting | bytes 4194304 | tf_op jit(solution)/shard_map/reshape | solution.py:52
  14.5 4.0 %reshape.96 = bf16[16,128,4,128]{3,2,1,0:T(4,128)(2,1)} reshape(bf16[2048,512]{1,0:T(8,128)(2,1)} %param.8) | data formatting | bytes 4194304 | tf_op jit(solution)/shard_map/reshape | solution.py:52
  18.4 3.1 %fusion.61 = (bf16[4,128,128]{2,1,0:T(8,128)(2,1)S(1)}, f32[16,4,128,128]{3,2,1,0:T(8,128)S(1)}) fusion(bf16[16,128,4,128]{3,2,1,0:T(4,128)(2,1)} %reshape.96, bf16[16,128,4,128]{3,2,1,0:T(4,128)(2,1)} %reshape.95), kind=kOutput, calls=%fused_computation.99 | convolution fusion | flops 269418496 | bytes 8519680 | tf_op jit(solution)/shard_map/cshe,cshf->chef/dot_general | solution.py:63
  21.6 6.4 %fusion.63 = f32[16,4,128,128]{3,2,1,0:T(8,128)S(1)} fusion(f32[16,4,128,128]{3,2,1,0:T(8,128)S(1)} %get-tuple-element.17), kind=kOutput, calls=%fused_computation.101 | output fusion | flops 15728640 | bytes 8388608 | tf_op jit(solution)/shard_map/jit(cumsum)/reduce_window_sum | solution.py:67
  28.0 0.4 slice.106
  28.5 0.0 copy-start.4
  28.5 2.1 all-gather
  30.7 14.4 %all_gather.28 = bf16[4,4,128,128]{3,2,1,0:T(8,128)(2,1)S(1)} all-gather(bf16[1,4,128,128]{3,2,1,0:T(8,128)(2,1)S(1)} %fusion.52), channel_id=1, replica_groups=mesh['ctx_0'=4,'ctx_1'=4,'ctx_2'=2,'head'=4] {'ctx_1'}, dimensions={0}, use_global_device_ids=true | all-gather | bytes 655360 | tf_op jit(solution)/shard_map/all_gather | solution.py:23
  45.1 0.1 fusion.51
  45.2 13.4 %all_gather.29 = bf16[4,4,128,128]{3,2,1,0:T(8,128)(2,1)S(1)} all-gather(bf16[1,4,128,128]{3,2,1,0:T(8,128)(2,1)S(1)} %fusion.51), channel_id=1, replica_groups=mesh['ctx_0'=4,'ctx_1'=4,'ctx_2'=2,'head'=4] {'ctx_0'}, dimensions={0}, use_global_device_ids=true | all-gather | bytes 655360 | tf_op jit(solution)/shard_map/all_gather | solution.py:23
  58.6 0.3 fusion.31
  58.8 0.0 copy-start.7
  58.8 1.6 select_convert_fusion.1
  60.4 1.3 copy-done.14
  61.7 0.7 fusion.14
  62.4 3.5 %multiply_reduce_fusion = (f32[16,128,4]{1,2,0:T(4,128)S(1)}, f32[16,128,4,128]{3,1,2,0:T(8,128)}) fusion(f32[15,4,128,128]{3,2,1,0:T(8,128)S(1)} %slice.106, f32[4,128,128]{2,1,0:T(8,128)S(1)} %fusion.31, bf16[16,128,4,128]{3,2,1,0:T(4,128)(2,1)S(1)} %reshape.94, f32[16,4,128,128]{3,2,1,0:T(8,128)S(1)} %fusion.14), kind=kOutput, calls=%fused_computation.16 | convolution fusion | flops 273670144 | bytes 14712832 | tf_op jit(solution)/shard_map/cshe,chef->cshf/dot_general | solution.py:71
  65.9 5.7 %copy.66 = f32[16,128,4,128]{1,0,3,2:T(8,128)} copy(f32[16,128,4,128]{3,1,2,0:T(8,128)} %get-tuple-element.19) | data formatting | bytes 8388608 | tf_op jit(solution)/shard_map/add | solution.py:71
  71.6 4.0 %fusion.1 = bf16[2048,512]{0,1:T(8,128)(2,1)S(1)} fusion(f32[64,8,16,128]{3,2,1,0:T(8,128)} %bitcast.93, f32[2048,4]{0,1:T(4,128)S(1)} %get-tuple-element.13, f32[512]{0:T(512)S(1)} %get-tuple-element.15), kind=kLoop, calls=%fused_computation.3 | loop fusion | flops 3145728 | bytes 6326272 | tf_op jit(solution)/shard_map/convert_element_type | solution.py:78
  75.6 8.4 %convolution_convert_fusion = bf16[2048,2048]{1,0:T(8,128)(2,1)} fusion(bf16[2048,512]{0,1:T(8,128)(2,1)S(1)} %fusion.1, bf16[2048,2048]{1,0:T(8,128)(2,1)} %param.10, s32[]{:T(128)S(6)} %select_n.175), kind=kOutput, calls=%fused_computation | convolution fusion | flops 4299161600 | bytes 12582916 | tf_op jit(solution)/shard_map/dot_general | solution.py:81
  84.0 0.0 reduce-scatter.2.cloned.1.call-update
  84.0 4.7 %copy.70 = f32[16,128,4,128]{3,1,0,2:T(8,128)} copy(f32[16,128,4,128]{3,1,2,0:T(8,128)} %get-tuple-element.19) | data formatting | bytes 8388608 | tf_op jit(solution)/shard_map/add | solution.py:71
  88.7 6.5 %all-gather.4.cloned.1.call-done = bf16[2048,2048]{1,0:T(8,128)(2,1)} async-done(((bf16[512,2048]{1,0:T(8,128)(2,1)}), bf16[2048,2048]{1,0:T(8,128)(2,1)}) %all-gather.4.cloned.1.call-update) | async-done | bytes 8388624 | tf_op jit(solution)/shard_map/all_gather | solution.py:87
  95.2 7.6 %fusion.6 = f32[512,2048]{1,0:T(8,128)S(1)} fusion(bf16[2048,2048]{1,0:T(8,128)(2,1)} %all-gather.4.cloned.1.call-done, bf16[2048,2048]{1,0:T(8,128)(2,1)} %param.10, s32[]{:T(128)S(6)} %select_n.175), kind=kOutput, calls=%fused_computation.20 | convolution fusion | flops 4297064448 | bytes 14680068 | tf_op jit(solution)/shard_map/dot_general | solution.py:86
  102.8 3.2 %copy.106 = f32[64,8,16,128]{3,2,1,0:T(8,128)} copy(f32[64,8,16,128]{3,1,2,0:T(8,128)S(1)} %bitcast.94) | data formatting | bytes 8388608
  106.1 5.3 %copy.68 = f32[16,128,4,128]{3,1,2,0:T(8,128)} copy(f32[16,128,4,128]{1,0,3,2:T(8,128)} %bitcast.96) | data formatting | bytes 8388608 | tf_op jit(solution)/shard_map/reshape | solution.py:92
  111.4 5.3 %copy.69 = f32[2048,4,128]{2,0,1:T(8,128)} copy(f32[2048,4,128]{0,2,1:T(8,128)} %bitcast.95) | data formatting | bytes 8388608 | tf_op jit(solution)/shard_map/reshape | solution.py:92
  116.7 4.9 %fusion.5 = f32[2048,4]{0,1:T(4,128)S(1)} fusion(f32[16,128,4,128]{3,1,0,2:T(8,128)} %copy.70, f32[2048,4,128]{2,0,1:T(8,128)} %copy.69, f32[4,128]{1,0:T(4,128)S(1)} %get-tuple-element.14, f32[2048,4]{0,1:T(4,128)S(1)} %get-tuple-element.13), kind=kLoop, calls=%fused_computation.10 | loop fusion | flops 4186112 | bytes 8456192 | tf_op jit(solution)/shard_map/reduce_sum | solution.py:94
  121.6 1.2 copy-done.12
  122.8 2.7 %multiply_convert_fusion = bf16[16,128,4,128]{3,1,2,0:T(8,128)(2,1)S(1)} fusion(f32[16,128,4,128]{3,1,2,0:T(8,128)S(1)} %copy-done, f32[16,128,4,128]{3,1,2,0:T(8,128)S(1)} %copy-done.12, f32[16,128,4]{1,2,0:T(4,128)S(1)} %multiply_bitcast_fusion, f32[4,128]{1,0:T(4,128)S(1)} %get-tuple-element.14, f32[16,128,4]{1,2,0:T(4,128)S(1)} %get-tuple-element.12), kind=kLoop, calls=%fused_computation.15 | loop fusion | flops 6291456 | bytes 10553344 | tf_op jit(solution)/shard_map/convert_element_type | solution.py:96
  125.6 1.6 select_convert_fusion
  127.2 1.3 copy-done.16
  128.5 0.7 fusion.18
  129.3 1.5 copy-done.2
  130.7 1.7 fusion.3
  132.4 1.8 copy.98
  134.2 1.7 copy.146
  135.9 2.9 %fusion.62 = (bf16[4,128,128]{1,2,0:T(8,128)(2,1)S(1)}, f32[16,4,128,128]{2,3,1,0:T(8,128)}) fusion(bf16[16,128,4,128]{3,1,2,0:T(8,128)(2,1)S(1)} %multiply_convert_fusion, bf16[16,128,4,128]{3,2,1,0:T(4,128)(2,1)S(1)} %reshape.94), kind=kOutput, calls=%fused_computation.100 | convolution fusion | flops 269418496 | bytes 8519680 | tf_op jit(solution)/shard_map/cshe,cshf->chef/dot_general | solution.py:100
  138.8 0.1 copy.80
  139.0 4.8 %rev.4 = f32[16,4,128,128]{2,3,1,0:T(8,128)} reverse(f32[16,4,128,128]{2,3,1,0:T(8,128)} %get-tuple-element.21), dimensions={0} | reverse | bytes 8388608 | tf_op jit(solution)/shard_map/rev | solution.py:104
  143.7 5.5 %copy.81 = f32[16,4,128,128]{3,2,1,0:T(8,128)} copy(f32[16,4,128,128]{2,3,1,0:T(8,128)} %rev.4) | data formatting | bytes 8388608 | tf_op jit(solution)/shard_map/rev | solution.py:104
  149.2 2.8 %fusion.64 = f32[16,4,128,128]{3,2,1,0:T(8,128)S(1)} fusion(f32[16,4,128,128]{3,2,1,0:T(8,128)} %copy.81), kind=kOutput, calls=%fused_computation.102 | output fusion | flops 15728640 | bytes 8388608 | tf_op jit(solution)/shard_map/jit(cumsum)/reduce_window_sum | solution.py:104
  152.0 2.3 %slice.117 = f32[15,4,128,128]{3,2,1,0:T(8,128)} slice(f32[16,4,128,128]{3,2,1,0:T(8,128)S(1)} %fusion.64), slice={[0:15], [0:4], [0:128], [0:128]} | slice | bytes 7864320 | tf_op jit(solution)/shard_map/slice | solution.py:105
  154.3 4.5 %slice.91 = f32[15,4,128,128]{3,2,1,0:T(8,128)} reverse(f32[15,4,128,128]{3,2,1,0:T(8,128)} %slice.117), dimensions={0} | reverse | bytes 7864320 | tf_op jit(solution)/shard_map/slice | solution.py:105
  158.8 2.1 all-gather.1
  161.0 13.3 %all_gather.32 = bf16[4,4,128,128]{3,2,1,0:T(8,128)(2,1)S(1)} all-gather(bf16[1,4,128,128]{3,2,1,0:T(8,128)(2,1)S(1)} %fusion.53), channel_id=1, replica_groups=mesh['ctx_0'=4,'ctx_1'=4,'ctx_2'=2,'head'=4] {'ctx_1'}, dimensions={0}, use_global_device_ids=true | all-gather | bytes 655360 | tf_op jit(solution)/shard_map/all_gather | solution.py:23
  174.2 0.1 fusion.50
  174.3 13.8 %all_gather.33 = bf16[4,4,128,128]{3,2,1,0:T(8,128)(2,1)S(1)} all-gather(bf16[1,4,128,128]{3,2,1,0:T(8,128)(2,1)S(1)} %fusion.50), channel_id=1, replica_groups=mesh['ctx_0'=4,'ctx_1'=4,'ctx_2'=2,'head'=4] {'ctx_0'}, dimensions={0}, use_global_device_ids=true | all-gather | bytes 655360 | tf_op jit(solution)/shard_map/all_gather | solution.py:23
  188.1 0.3 fusion.40
  188.4 0.0 copy-start.9
  188.4 0.9 fusion.22
  189.3 1.2 copy-done.3
  190.5 0.7 copy-done.9
  191.2 1.6 fusion.2
  192.8 1.8 copy.99
  194.6 0.4 copy-done.15
  195.0 0.9 fusion.65
  195.8 0.7 copy-done.6
  196.6 2.9 %fusion.9 = bf16[16,128,4,128]{1,3,2,0:T(8,128)(2,1)} fusion(f32[16,4,128,128]{3,2,1,0:T(8,128)S(1)} %fusion.65, bf16[16,128,4,128]{3,2,1,0:T(4,128)(2,1)S(1)} %copy-done.6, f32[15,4,128,128]{3,2,1,0:T(8,128)S(1)} %copy-done.3, f32[4,128,128]{2,1,0:T(8,128)S(1)} %fusion.40), kind=kOutput, calls=%fused_computation.27 | convolution fusion | flops 272629760 | bytes 12582912 | tf_op jit(solution)/shard_map/cthe,chef->cthf/dot_general | solution.py:120
  199.5 4.3 %copy.100 = bf16[16,128,4,128]{3,2,1,0:T(4,128)(2,1)} copy(bf16[16,128,4,128]{1,3,2,0:T(8,128)(2,1)} %fusion.9) | data formatting | bytes 4194304
  203.8 4.3 %copy_bitcast_fusion = (bf16[2048,512]{1,0:T(8,128)(2,1)}, bf16[2048,512]{1,0:T(8,128)(2,1)}) fusion(bf16[256,8,4,128]{3,2,1,0:T(4,128)(2,1)} %bitcast.99, bf16[256,8,4,128]{3,2,1,0:T(4,128)(2,1)S(1)} %bitcast.98), kind=kLoop, calls=%fused_computation.22 | loop fusion | bytes 8388608
  (34 shorter events, 0.2 us)
Async XLA Ops:
  7.2 88.0 %all-gather.4.cloned.1.call-start = ((), (), s32[]{:S(2)}) async-start(), calls=%async_computation.2 | async-start | bytes 10485760 | tf_op jit(solution)/shard_map/all_gather | solution.py:87
  7.9 200.2 %reduce-scatter.2.cloned.1.call-start = ((), (), s32[]{:S(2)}) async-start(), calls=%async_computation.1 | async-start | bytes 10485760 | tf_op jit(solution)/shard_map/reduce_scatter | solution.py:80
  28.5 34.0 %copy-start.1 = (f32[15,4,128,128]{3,2,1,0:T(8,128)}, f32[15,4,128,128]{3,2,1,0:T(8,128)S(1)}, u32[]{:S(2)}) copy-start(f32[15,4,128,128]{3,2,1,0:T(8,128)S(1)} %slice.106) | copy-start | bytes 11796484
  28.5 30.3 %copy-start.4 = (bf16[16,128,4,128]{3,2,1,0:T(4,128)(2,1)S(1)}, bf16[16,128,4,128]{3,2,1,0:T(4,128)(2,1)}, u32[]{:S(2)}) copy-start(bf16[16,128,4,128]{3,2,1,0:T(4,128)(2,1)} %reshape.95) | copy-start | bytes 6291460
  58.8 2.9 %copy-start.7 = (bf16[16,128,4,128]{3,2,1,0:T(4,128)(2,1)S(1)}, bf16[16,128,4,128]{3,2,1,0:T(4,128)(2,1)}, u32[]{:S(2)}) copy-start(bf16[16,128,4,128]{3,2,1,0:T(4,128)(2,1)} %reshape.96) | copy-start | bytes 6291460
  60.4 1.3 copy-start.14
  65.9 5.7 %copy-start.18 = (bf16[512]{0:T(512)(128)(2,1)S(1)}, bf16[512]{0:T(512)(128)(2,1)}, u32[]{:S(2)}) copy-start(bf16[512]{0:T(512)(128)(2,1)} %param.9) | copy-start | bytes 3076
  102.8 3.2 %copy-start.13 = (f32[512,2048]{1,0:T(8,128)}, f32[512,2048]{1,0:T(8,128)S(1)}, u32[]{:S(2)}) copy-start(f32[512,2048]{1,0:T(8,128)S(1)} %fusion.6) | copy-start | bytes 12582916
  116.7 4.9 %copy-start = (f32[16,128,4,128]{3,1,2,0:T(8,128)S(1)}, f32[16,128,4,128]{3,1,2,0:T(8,128)}, u32[]{:S(2)}) copy-start(f32[16,128,4,128]{3,1,2,0:T(8,128)} %get-tuple-element.19) | copy-start | bytes 12582916
  116.7 6.1 %copy-start.12 = (f32[16,128,4,128]{3,1,2,0:T(8,128)S(1)}, f32[16,128,4,128]{3,1,2,0:T(8,128)}, u32[]{:S(2)}) copy-start(f32[16,128,4,128]{3,1,2,0:T(8,128)} %copy.68) | copy-start | bytes 12582916
  122.8 2.8 %copy-start.8 = (bf16[16,128,4,128]{3,2,1,0:T(4,128)(2,1)S(1)}, bf16[16,128,4,128]{3,2,1,0:T(4,128)(2,1)}, u32[]{:S(2)}) copy-start(bf16[16,128,4,128]{3,2,1,0:T(4,128)(2,1)} %reshape.96) | copy-start | bytes 6291460
  125.6 10.3 %copy-start.10 = (bf16[16,128,4,128]{3,1,2,0:T(8,128)(2,1)}, bf16[16,128,4,128]{3,1,2,0:T(8,128)(2,1)S(1)}, u32[]{:S(2)}) copy-start(bf16[16,128,4,128]{3,1,2,0:T(8,128)(2,1)S(1)} %multiply_convert_fusion) | copy-start | bytes 6291460
  125.6 2.9 %copy-start.5 = (bf16[16,128,4,128]{3,2,1,0:T(4,128)(2,1)S(1)}, bf16[16,128,4,128]{3,2,1,0:T(4,128)(2,1)}, u32[]{:S(2)}) copy-start(bf16[16,128,4,128]{3,2,1,0:T(4,128)(2,1)} %reshape.95) | copy-start | bytes 6291460
  127.2 1.3 copy-start.16
  128.5 2.2 %copy-start.2 = (f32[15,4,128,128]{3,2,1,0:T(8,128)S(1)}, f32[15,4,128,128]{3,2,1,0:T(8,128)}, u32[]{:S(2)}) copy-start(f32[15,4,128,128]{3,2,1,0:T(8,128)} %copy-done.1) | copy-start | bytes 11796484
  158.8 29.6 %copy-start.17 = (bf16[16,4,128,128]{3,2,1,0:T(8,128)(2,1)S(1)}, bf16[16,4,128,128]{3,2,1,0:T(8,128)(2,1)}, u32[]{:S(2)}) copy-start(bf16[16,4,128,128]{3,2,1,0:T(8,128)(2,1)} %copy-done.16) | copy-start | bytes 6291460
  188.4 2.1 copy-start.3
  188.4 2.8 %copy-start.9 = (bf16[16,128,4,128]{3,2,1,0:T(4,128)(2,1)S(1)}, bf16[16,128,4,128]{3,2,1,0:T(4,128)(2,1)}, u32[]{:S(2)}) copy-start(bf16[16,128,4,128]{3,2,1,0:T(4,128)(2,1)} %reshape.96) | copy-start | bytes 6291460
  192.8 1.8 copy-start.11
  192.8 2.2 %copy-start.15 = (bf16[16,4,128,128]{3,2,1,0:T(8,128)(2,1)S(1)}, bf16[16,4,128,128]{3,2,1,0:T(8,128)(2,1)}, u32[]{:S(2)}) copy-start(bf16[16,4,128,128]{3,2,1,0:T(8,128)(2,1)} %copy-done.14) | copy-start | bytes 6291460
  195.0 1.6 copy-start.6
Sparse Core Ops, SparseCore 0:
  9.6 85.5 all-gather.3
  98.2 81.4 reduce-scatter.1
where the time goes:
time: 216 us; the launch traced here: 215 us
  local copies, waits for them, and re-layouts  74.5 us (34%)
  blocking collectives  59.1 us (27%)
  matrix products  38 us (18%)
  other arithmetic  21.5 us (10%)
  between operations  14.4 us (7%)
  waiting for transfers between devices  7.24 us (3%)
    all_gather x6, blocking collectives, prefix_by_axis(): pieces = lax.all_gather(total.astype(jnp.bfloat16), axis)  59.1 us
    unnamed x44, local copies, waits for them, and re-layouts  25.4 us
    reshape x2, local copies, waits for them, and re-layouts, on_device(): grad_heads.astype(jnp.float32).reshape(tokens, local_heads, HDIM) * scales  10.7 us
    reshape x3, local copies, waits for them, and re-layouts, split_blocks(): return array.reshape(nblocks, BLOCK, local_heads, HDIM)  10.5 us
    add x2, local copies, waits for them, and re-layouts, on_device(): attended + jnp.einsum('cshe,chef->cshf', q_blocks, prefixes, preferred_el...  10.3 us
    rev x2, local copies, waits for them, and re-layouts, on_device(): tail_sums = jnp.cumsum(block_grads[::-1], axis=0)[::-1]  10.3 us
    dot_general x1, matrix products, on_device(): jnp.dot(normed, w_slice, preferred_element_type=jnp.float32)  8.4 us
    dot_general x1, matrix products, on_device(): lax.dot_general(lax.all_gather(d_out, 'head', axis=0, tiled=True), w_slic...  7.63 us
  transfers between devices with their start and end apart: 2, of which 1 were waited for; matrix products, arithmetic and copies ran while one was open for 58% of the time, Pallas kernels for 0%

commit v1 on v0

--- a/solution.py
+++ b/solution.py
@@ -84,7 +84,9 @@
         tiled=True,
     )
     grad_heads = lax.dot_general(
-        lax.all_gather(d_out, "head", axis=0, tiled=True),
+        jnp.concatenate(
+            lax.all_to_all(jnp.stack([d_out] * lax.axis_size("head")), "head", 0, 0), axis=0
+        ),
         w_slice,
         (((1,), (1,)), ((), ())),
         preferred_element_type=jnp.float32,

time: 216 us -> 375 us (1.74)
  waiting for transfers between devices: 7.24 us -> 153 us
  starting transfers between devices: 0.08 us -> 5.89 us
  local copies, waits for them, and re-layouts: 74.5 us -> 79.6 us
    all_to_all x0 -> x1, waiting for transfers between devices: none -> 153 us  [on_device(): lax.all_to_all(jnp.stack([d_out] * lax.axis_size('head')), 'head', 0, 0)]
    all_gather x1 -> x0, waiting for transfers between devices: 6.54 us -> none  [on_device(): lax.all_gather(d_out, 'head', axis=0, tiled=True)]
    another operation x0 -> x1, local copies, waits for them, and re-layouts: none -> 5.9 us  [on_device(): jnp.stack([d_out] * lax.axis_size('head'))]
    all_to_all x0 -> x1, starting transfers between devices: none -> 5.85 us  [on_device(): lax.all_to_all(jnp.stack([d_out] * lax.axis_size('head')), 'head', 0, 0)]
    unnamed x44 -> x48, local copies, waits for them, and re-layouts: 25.4 us -> 24.3 us
  transfers between devices with their start and end apart: 2 -> 2, of which waited for: 1 -> 1; matrix products, arithmetic and copies ran while one was open for 58% -> 23% of each run, Pallas kernels for 0% -> 0%
where the time goes in v1:
time: 375 us; the launch traced here: 374 us
  waiting for transfers between devices  153 us (41%)
  local copies, waits for them, and re-layouts  79.6 us (21%)
  blocking collectives  58.8 us (16%)
  matrix products  40.8 us (11%)
  other arithmetic  21.2 us (6%)
  between operations  14.4 us (4%)
  starting transfers between devices  5.89 us (2%)
    all_to_all x1, waiting for transfers between devices, on_device(): lax.all_to_all(jnp.stack([d_out] * lax.axis_size('head')), 'head', 0, 0)  153 us
    all_gather x6, blocking collectives, prefix_by_axis(): pieces = lax.all_gather(total.astype(jnp.bfloat16), axis)  58.8 us
    unnamed x48, local copies, waits for them, and re-layouts  24.3 us
    reshape x2, local copies, waits for them, and re-layouts, on_device(): grad_heads.astype(jnp.float32).reshape(tokens, local_heads, HDIM) * scales  10.6 us
    add x2, local copies, waits for them, and re-layouts, on_device(): attended + jnp.einsum('cshe,chef->cshf', q_blocks, prefixes, preferred_el...  10.1 us
    rev x2, local copies, waits for them, and re-layouts, on_device(): tail_sums = jnp.cumsum(block_grads[::-1], axis=0)[::-1]  9.99 us
    reshape x3, local copies, waits for them, and re-layouts, split_blocks(): return array.reshape(nblocks, BLOCK, local_heads, HDIM)  9.44 us
    dot_general x1, matrix products, on_device(): jnp.dot(normed, w_slice, preferred_element_type=jnp.float32)  8.37 us
  transfers between devices with their start and end apart: 2, of which 1 were waited for; matrix products, arithmetic and copies ran while one was open for 23% of the time, Pallas kernels for 0%

profile of v1, /device:TPU:0, one launch (start us, length us, event | category | flops | bytes accessed | tf_op | source)
XLA Modules:
  0.0 373.9 jit_solution(15603049400353060921)
XLA Ops:
  7.2 0.0 reduce-scatter.2.cloned.1.call-start
  7.3 2.6 reshape.101
  9.8 0.0 copy-start.5
  9.8 4.3 %reshape.100 = bf16[16,128,4,128]{3,2,1,0:T(4,128)(2,1)} reshape(bf16[2048,512]{1,0:T(8,128)(2,1)} %param.7) | data formatting | bytes 4194304 | tf_op jit(solution)/shard_map/reshape | solution.py:52
  14.2 2.5 fusion.61
  16.7 6.4 %fusion.63 = f32[16,4,128,128]{3,2,1,0:T(8,128)S(1)} fusion(f32[16,4,128,128]{3,2,1,0:T(8,128)S(1)} %get-tuple-element.17), kind=kOutput, calls=%fused_computation.101 | output fusion | flops 15728640 | bytes 8388608 | tf_op jit(solution)/shard_map/jit(cumsum)/reduce_window_sum | solution.py:67
  23.1 2.4 slice.106
  25.6 2.0 all-gather
  27.6 14.1 %all_gather.25 = bf16[4,4,128,128]{3,2,1,0:T(8,128)(2,1)S(1)} all-gather(bf16[1,4,128,128]{3,2,1,0:T(8,128)(2,1)S(1)} %fusion.52), channel_id=1, replica_groups=mesh['ctx_0'=4,'ctx_1'=4,'ctx_2'=2,'head'=4] {'ctx_1'}, dimensions={0}, use_global_device_ids=true | all-gather | bytes 655360 | tf_op jit(solution)/shard_map/all_gather | solution.py:23
  41.7 0.1 fusion.51
  41.8 14.3 %all_gather.26 = bf16[4,4,128,128]{3,2,1,0:T(8,128)(2,1)} all-gather(bf16[1,4,128,128]{3,2,1,0:T(8,128)(2,1)S(1)} %fusion.51), channel_id=1, replica_groups=mesh['ctx_0'=4,'ctx_1'=4,'ctx_2'=2,'head'=4] {'ctx_0'}, dimensions={0}, use_global_device_ids=true | all-gather | bytes 655360 | tf_op jit(solution)/shard_map/all_gather | solution.py:23
  56.0 2.5 reshape.99
  58.6 3.3 select_convert_fusion.1
  61.9 0.7 fusion.14
  62.7 0.6 copy-done.16
  63.2 0.1 copy-done.19
  63.3 0.3 fusion.31
  63.6 1.4 copy-done.1
  65.0 3.5 multiply_reduce_fusion
  68.4 5.5 %copy.66 = f32[16,128,4,128]{1,0,3,2:T(8,128)} copy(f32[16,128,4,128]{3,1,2,0:T(8,128)} %get-tuple-element.19) | data formatting | bytes 8388608 | tf_op jit(solution)/shard_map/add | solution.py:71
  74.0 4.0 %fusion.1 = bf16[2048,512]{0,1:T(8,128)(2,1)S(1)} fusion(f32[64,8,16,128]{3,2,1,0:T(8,128)} %bitcast.94, f32[2048,4]{0,1:T(4,128)S(1)} %get-tuple-element.13, f32[512]{0:T(512)S(1)} %get-tuple-element.15), kind=kLoop, calls=%fused_computation.3 | loop fusion | flops 3145728 | bytes 6326272 | tf_op jit(solution)/shard_map/convert_element_type | solution.py:78
  77.9 8.4 %convolution_convert_fusion = bf16[2048,2048]{1,0:T(8,128)(2,1)} fusion(bf16[2048,512]{0,1:T(8,128)(2,1)S(1)} %fusion.1, bf16[2048,2048]{1,0:T(8,128)(2,1)} %param.10, s32[]{:T(128)S(6)} %select_n.175), kind=kOutput, calls=%fused_computation | convolution fusion | flops 4299161600 | bytes 12582916 | tf_op jit(solution)/shard_map/dot_general | solution.py:81
  86.3 0.0 reduce-scatter.2.cloned.1.call-update
  86.3 5.9 %stack.2 = bf16[4,512,2048]{2,1,0:T(8,128)(2,1)} broadcast(bf16[512,2048]{1,0:T(8,128)(2,1)} %param.11), dimensions={1,2} | broadcast | bytes 10485760 | tf_op jit(solution)/shard_map/stack | solution.py:88
  92.2 5.9 %all-to-all-start = ((bf16[4,512,2048]{2,1,0:T(8,128)(2,1)}), bf16[4,512,2048]{2,1,0:T(8,128)(2,1)}, u32[]{:S(2)}, u32[]{:S(2)}) async-start(bf16[4,512,2048]{2,1,0:T(8,128)(2,1)} %stack.2), calls=%async_computation.1 | async-start | bytes 16777216 | tf_op jit(solution)/shard_map/all_to_all | solution.py:88
  98.1 4.6 %copy.70 = f32[16,128,4,128]{3,1,0,2:T(8,128)} copy(f32[16,128,4,128]{3,1,2,0:T(8,128)} %get-tuple-element.19) | data formatting | bytes 8388608 | tf_op jit(solution)/shard_map/add | solution.py:71
  102.7 153.0 %all-to-all-done = bf16[4,512,2048]{2,1,0:T(8,128)(2,1)} async-done(((bf16[4,512,2048]{2,1,0:T(8,128)(2,1)}), bf16[4,512,2048]{2,1,0:T(8,128)(2,1)}, u32[]{:S(2)}, u32[]{:S(2)}) %all-to-all-start) | async-done | bytes 8388640 | tf_op jit(solution)/shard_map/all_to_all | solution.py:88
  255.7 7.6 %fusion.6 = f32[512,2048]{1,0:T(8,128)S(1)} fusion(bf16[2048,2048]{1,0:T(8,128)(2,1)} %bitcast.7, bf16[2048,2048]{1,0:T(8,128)(2,1)} %param.10, s32[]{:T(128)S(6)} %select_n.175), kind=kOutput, calls=%fused_computation.20 | convolution fusion | flops 4297064448 | bytes 14680068 | tf_op jit(solution)/shard_map/dot_general | solution.py:86
  263.4 3.2 copy.106
  266.6 5.2 %copy.68 = f32[16,128,4,128]{3,1,2,0:T(8,128)} copy(f32[16,128,4,128]{1,0,3,2:T(8,128)} %bitcast.97) | data formatting | bytes 8388608 | tf_op jit(solution)/shard_map/reshape | solution.py:94
  271.8 5.3 %copy.69 = f32[2048,4,128]{2,0,1:T(8,128)} copy(f32[2048,4,128]{0,2,1:T(8,128)} %bitcast.96) | data formatting | bytes 8388608 | tf_op jit(solution)/shard_map/reshape | solution.py:94
  277.2 4.8 %fusion.5 = f32[2048,4]{0,1:T(4,128)S(1)} fusion(f32[16,128,4,128]{3,1,0,2:T(8,128)} %copy.70, f32[2048,4,128]{2,0,1:T(8,128)} %copy.69, f32[4,128]{1,0:T(4,128)S(1)} %get-tuple-element.14, f32[2048,4]{0,1:T(4,128)S(1)} %get-tuple-element.13), kind=kLoop, calls=%fused_computation.10 | loop fusion | flops 4186112 | bytes 8456192 | tf_op jit(solution)/shard_map/reduce_sum | solution.py:96
  282.0 1.1 copy-done.13
  283.1 2.5 multiply_convert_fusion
  285.7 1.6 select_convert_fusion
  287.2 1.3 copy-done.18
  288.6 0.7 fusion.18
  289.3 1.4 copy-done.2
  290.7 1.7 fusion.3
  292.4 1.8 copy.98
  294.1 1.7 copy.146
  295.8 2.9 fusion.62
  298.8 4.6 %rev.4 = f32[16,4,128,128]{2,3,1,0:T(8,128)} reverse(f32[16,4,128,128]{2,3,1,0:T(8,128)} %get-tuple-element.21), dimensions={0} | reverse | bytes 8388608 | tf_op jit(solution)/shard_map/rev | solution.py:106
  303.4 5.3 %copy.81 = f32[16,4,128,128]{3,2,1,0:T(8,128)} copy(f32[16,4,128,128]{2,3,1,0:T(8,128)} %rev.4) | data formatting | bytes 8388608 | tf_op jit(solution)/shard_map/rev | solution.py:106
  308.7 2.7 fusion.64
  311.5 2.3 slice.117
  313.8 4.4 %slice.91 = f32[15,4,128,128]{3,2,1,0:T(8,128)} reverse(f32[15,4,128,128]{3,2,1,0:T(8,128)} %slice.117), dimensions={0} | reverse | bytes 7864320 | tf_op jit(solution)/shard_map/slice | solution.py:107
  318.3 0.1 copy.80
  318.4 2.1 all-gather.1
  320.6 13.4 %all_gather.28 = bf16[4,4,128,128]{3,2,1,0:T(8,128)(2,1)S(1)} all-gather(bf16[1,4,128,128]{3,2,1,0:T(8,128)(2,1)S(1)} %fusion.53), channel_id=1, replica_groups=mesh['ctx_0'=4,'ctx_1'=4,'ctx_2'=2,'head'=4] {'ctx_1'}, dimensions={0}, use_global_device_ids=true | all-gather | bytes 655360 | tf_op jit(solution)/shard_map/all_gather | solution.py:23
  334.0 0.1 fusion.50
  334.1 12.9 %all_gather.29 = bf16[4,4,128,128]{3,2,1,0:T(8,128)(2,1)S(1)} all-gather(bf16[1,4,128,128]{3,2,1,0:T(8,128)(2,1)S(1)} %fusion.50), channel_id=1, replica_groups=mesh['ctx_0'=4,'ctx_1'=4,'ctx_2'=2,'head'=4] {'ctx_0'}, dimensions={0}, use_global_device_ids=true | all-gather | bytes 655360 | tf_op jit(solution)/shard_map/all_gather | solution.py:23
  347.1 0.3 fusion.40
  347.4 0.9 fusion.65
  348.2 1.2 copy-done.3
  349.4 0.7 copy-done.10
  350.1 2.9 fusion.9
  353.0 4.3 %copy.100 = bf16[16,128,4,128]{3,2,1,0:T(4,128)(2,1)} copy(bf16[16,128,4,128]{1,3,2,0:T(8,128)(2,1)} %fusion.9) | data formatting | bytes 4194304
  357.3 2.6 fusion.22
  359.9 0.1 copy-done.4
  360.1 0.7 copy-done.8
  360.7 1.6 fusion.2
  362.3 1.8 copy.99
  364.1 3.0 copy_bitcast_fusion
  (38 shorter events, 0.2 us)
Async XLA Ops:
  7.2 359.9 %reduce-scatter.2.cloned.1.call-start = ((), (), s32[]{:S(2)}) async-start(), calls=%async_computation.2 | async-start | bytes 10485760 | tf_op jit(solution)/shard_map/reduce_scatter | solution.py:80
  9.8 4.4 %copy-start.5 = (bf16[16,128,4,128]{3,2,1,0:T(4,128)(2,1)}, bf16[16,128,4,128]{3,2,1,0:T(4,128)(2,1)S(1)}, u32[]{:S(2)}) copy-start(bf16[16,128,4,128]{3,2,1,0:T(4,128)(2,1)S(1)} %reshape.101) | copy-start | bytes 6291460
  58.6 3.3 copy-start.6
  61.9 1.3 copy-start.16
  61.9 1.4 copy-start.19
  61.9 3.0 copy-start.1
  68.4 5.5 %copy-start.20 = (bf16[512]{0:T(512)(128)(2,1)S(1)}, bf16[512]{0:T(512)(128)(2,1)}, u32[]{:S(2)}) copy-start(bf16[512]{0:T(512)(128)(2,1)} %param.9) | copy-start | bytes 3076
  92.2 163.5 %all-to-all-start = ((bf16[4,512,2048]{2,1,0:T(8,128)(2,1)}), bf16[4,512,2048]{2,1,0:T(8,128)(2,1)}, u32[]{:S(2)}, u32[]{:S(2)}) async-start(bf16[4,512,2048]{2,1,0:T(8,128)(2,1)} %stack.2), calls=%async_computation.1 | async-start | bytes 16777216 | tf_op jit(solution)/shard_map/all_to_all | solution.py:88
  263.4 3.2 copy-start.14
  277.2 4.8 %copy-start = (f32[16,128,4,128]{3,1,2,0:T(8,128)S(1)}, f32[16,128,4,128]{3,1,2,0:T(8,128)}, u32[]{:S(2)}) copy-start(f32[16,128,4,128]{3,1,2,0:T(8,128)} %get-tuple-element.19) | copy-start | bytes 12582916
  277.2 5.9 %copy-start.13 = (f32[16,128,4,128]{3,1,2,0:T(8,128)S(1)}, f32[16,128,4,128]{3,1,2,0:T(8,128)}, u32[]{:S(2)}) copy-start(f32[16,128,4,128]{3,1,2,0:T(8,128)} %copy.68) | copy-start | bytes 12582916
  283.1 2.5 copy-start.7
  285.6 10.2 %copy-start.11 = (bf16[16,128,4,128]{3,1,2,0:T(8,128)(2,1)}, bf16[16,128,4,128]{3,1,2,0:T(8,128)(2,1)S(1)}, u32[]{:S(2)}) copy-start(bf16[16,128,4,128]{3,1,2,0:T(8,128)(2,1)S(1)} %multiply_convert_fusion) | copy-start | bytes 6291460
  285.6 2.9 copy-start.9
  287.2 1.3 copy-start.18
  288.6 2.1 copy-start.2
  318.4 28.9 %copy-start.12 = (bf16[16,128,4,128]{3,1,2,0:T(8,128)(2,1)S(1)}, bf16[16,128,4,128]{3,1,2,0:T(8,128)(2,1)}, u32[]{:S(2)}) copy-start(bf16[16,128,4,128]{3,1,2,0:T(8,128)(2,1)} %copy-done.11) | copy-start | bytes 6291460
  318.4 28.9 %copy-start.17 = (bf16[16,4,128,128]{3,2,1,0:T(8,128)(2,1)S(1)}, bf16[16,4,128,128]{3,2,1,0:T(8,128)(2,1)}, u32[]{:S(2)}) copy-start(bf16[16,4,128,128]{3,2,1,0:T(8,128)(2,1)} %copy-done.16) | copy-start | bytes 6291460
  347.3 2.1 copy-start.3
  347.3 2.8 copy-start.10
  357.3 2.7 copy-start.4
  357.3 3.4 copy-start.8
  362.3 1.8 copy-start.15
Sparse Core Ops, SparseCore 0:
  86.4 147.3 reduce-scatter.1
